TPU v7x, 128 devices: a whole 4x4x4 slice. The times are simulated.
128 devices in a mesh: lat: 32 (over z, x, core), lev: 4 (over y).
Axes of the slice: x: 4, y: 4, z: 4, core: 2. Of those that a mesh axis runs over, the one named last changes fastest.
Arguments:
- grid: bfloat16 [640, 128, 4, 1280], P('lat', 'lev'), may hold values from -6 to 6
- legendre: bfloat16 [640, 640, 640], P('lat'), may hold values from -0.25 to 0.25
- vertical: bfloat16 [128, 128], P('lev'), may hold values from -0.5 to 0.5
- damping: bfloat16 [128], P('lev'), may hold values from 1 to 16
- lon_counts: int32 [640], replicated, may hold values from 160 to 1280
- wave_slots: int32 [640], replicated, may hold values from 0 to 639, as said below
Outputs:
- filtered_grid: bfloat16 [640, 128, 4, 1280], P('lat', 'lev')
Inputs may be any that keep to these rules, and one draw needn't show every extreme that they name: wave_slots is a permutation; slot g * 5 + r holds a wavenumber from r * 128 to (r + 1) * 128 - 1.
All inputs are finite; a program needn't handle non-finite values.
Results may differ from a plain program's by a relative error of at most 0.0074.
Values may be sent and summed in bfloat16 or wider, within the bound.
A program may use at most 128 MiB of HBM per device.

v0:
```python
import math
import jax
import jax.numpy as jnp
from jax import lax
from jax.sharding import PartitionSpec as P


def sent_together(arrays, axis, dim, along):
    widths = [math.prod(a.shape[along:]) for a in arrays]
    both = jnp.concatenate(
        [a.reshape(*a.shape[:along], w) for a, w in zip(arrays, widths)], axis=along
    )
    result = lax.all_gather(both, axis, axis=dim, tiled=True)
    pieces = jnp.split(result, [sum(widths[:k]) for k in range(1, len(widths))], axis=along)
    return tuple(
        (b.reshape(*result.shape[:along], *a.shape[along:]) for a, b in zip(arrays, pieces))
    )


def in_blocks(array, dim, peers):
    before, after = (array.shape[:dim], array.shape[dim + 1 :])
    return jnp.moveaxis(array.reshape(*before, peers, -1, *after), dim, 0)


def in_order(pieces, dim):
    lengths = list(pieces.shape[1:])
    lengths[dim] *= pieces.shape[0]
    return jnp.moveaxis(pieces, 0, dim).reshape(lengths)


def joined_exchange(array, axis, axes, splits, concats):
    sizes = [lax.axis_size(a) for a in axes]
    pieces = in_blocks(array, splits[0], sizes[0])
    pieces = jnp.moveaxis(in_blocks(pieces, splits[1] + 1, sizes[1]), 0, 1)
    inside = pieces.shape[2:]
    pieces = pieces.reshape(-1, *inside)
    pieces = lax.all_to_all(pieces, axis, split_axis=0, concat_axis=0, tiled=True)
    pieces = in_order(pieces.reshape(*sizes, *inside), concats[0] + 1)
    return in_order(pieces, concats[1])


def forward_build(wavenumbers, longitudes):
    points = jnp.arange(longitudes, dtype=jnp.int32)
    phase = (wavenumbers[:, None] * points[None, :] % longitudes).astype(jnp.float32) * (
        2.0 * math.pi / longitudes
    )
    scale = 1.0 / math.sqrt(longitudes)
    return jnp.stack([jnp.cos(phase) * scale, -jnp.sin(phase) * scale], axis=1).astype(jnp.bfloat16)


def inverse_build(wavenumbers, longitudes):
    points = jnp.arange(longitudes, dtype=jnp.int32)
    phase = (wavenumbers[:, None] * points[None, :] % longitudes).astype(jnp.float32) * (
        2.0 * math.pi / longitudes
    )
    scale = 1.0 / math.sqrt(longitudes)
    weight = jnp.where(wavenumbers == 0, 1.0, 2.0).astype(jnp.float32)[:, None]
    return jnp.stack(
        [jnp.cos(phase) * scale * weight, -jnp.sin(phase) * scale * weight], axis=1
    ).astype(jnp.bfloat16)


def damping_factor(degrees, damping):
    degree_values = jnp.arange(degrees).astype(jnp.float32)
    ratio = degree_values * (degree_values + 1.0) / float(degrees * (degrees - 1))
    return 1.0 / (1.0 + damping.astype(jnp.float32)[None, :] * (ratio * ratio)[:, None])


def legendre_forward(table, fourier, wavenumbers):
    degrees = table.shape[1]
    spectral = jnp.einsum("sna,srac->snrc", table, fourier, preferred_element_type=jnp.float32)
    live = (jnp.arange(degrees, dtype=jnp.int32)[None, :] >= wavenumbers[:, None]).astype(
        jnp.float32
    )
    return (spectral * live[:, :, None, None]).astype(jnp.bfloat16)


def legendre_inverse(table, mixed):
    banded = jnp.einsum("sna,snrc->srac", table, mixed, preferred_element_type=jnp.float32)
    return banded.astype(jnp.bfloat16)


def per_device(grid, legendre, vertical, damping, lon_counts, wave_slots):
    lat_rows, level_rows, fields, longitudes = grid.shape
    slot_count = wave_slots.shape[0]
    degrees = legendre.shape[1]
    own_slots = legendre.shape[0]
    forward_table = forward_build(wave_slots, longitudes)
    own_counts = lax.dynamic_slice_in_dim(lon_counts, lax.axis_index("lat") * lat_rows, lat_rows)
    fourier = jnp.einsum("mrx,alfx->mralf", forward_table, grid, preferred_element_type=jnp.float32)
    fourier = fourier.reshape(slot_count, 2, lat_rows, level_rows * fields)
    forward_kept = (2 * wave_slots[:, None] < own_counts[None, :]).astype(jnp.float32)
    fourier = (fourier * forward_kept[:, None, :, None]).astype(jnp.bfloat16)
    gathered = lax.all_to_all(
        lax.all_to_all(fourier, "lat", split_axis=0, concat_axis=2, tiled=True),
        "lev",
        split_axis=0,
        concat_axis=3,
        tiled=True,
    )
    count = gathered.shape[0]
    own_table = lax.dynamic_slice_in_dim(legendre, lax.axis_index("lev") * count, count, 0)
    own_waves = lax.dynamic_slice_in_dim(
        wave_slots, lax.axis_index("lat") * own_slots + lax.axis_index("lev") * count, count
    )
    spectral = legendre_forward(own_table, gathered, own_waves)
    all_rows, all_damping = sent_together((vertical, damping), "lev", 0, 1)
    levels = all_rows.shape[0]
    stacked = spectral.reshape(count, degrees, 2, levels, fields)
    mixed = stacked.astype(jnp.float32) + jnp.einsum(
        "snrkf,lk->snrlf", stacked, all_rows, preferred_element_type=jnp.float32
    )
    mixed = mixed * damping_factor(degrees, all_damping)[None, :, None, :, None]
    mixed = mixed.astype(jnp.bfloat16).reshape(count, degrees, 2, levels * fields)
    banded = legendre_inverse(own_table, mixed)
    returned = joined_exchange(banded, ("lat", "lev"), ("lat", "lev"), (2, 3), (0, 0))
    back_order = (
        wave_slots.reshape(lax.axis_size("lat"), lax.axis_size("lev"), count)
        .transpose(1, 0, 2)
        .reshape(slot_count)
    )
    inverse_table = inverse_build(back_order, longitudes)
    back_kept = (2 * back_order[:, None] < own_counts[None, :]).astype(jnp.bfloat16)
    returned = returned * back_kept[:, None, :, None]
    filtered_grid = jnp.einsum(
        "mrac,mrx->acx", returned, inverse_table, preferred_element_type=jnp.float32
    )
    return filtered_grid.reshape(lat_rows, level_rows, fields, longitudes).astype(jnp.bfloat16)


def solution(mesh):
    return jax.shard_map(
        per_device,
        mesh=mesh,
        in_specs=(
            P("lat", "lev", None, None),
            P("lat", None, None),
            P("lev", None),
            P("lev"),
            P(),
            P(),
        ),
        out_specs=P("lat", "lev", None, None),
        check_vma=False,
    )
```

profile of v0, /device:TPU:3, one launch (start us, length us, event | category | flops | bytes accessed | tf_op | source)
XLA Modules:
  0.0 534.7 jit_solution(11057568427985806592)
XLA Ops:
  0.0 15.9 %multiply_convert_fusion.5 = (bf16[640,1,1280]{2,0,1:T(8,128)(2,1)S(1)}, bf16[640,1,1280]{2,0,1:T(8,128)(2,1)S(1)}) fusion(s32[640]{0:T(1024)} %param.11), kind=kLoop, calls=%fused_computation.38 | loop fusion | flops 11468800 | bytes 3279360 | tf_op jit(solution)/shard_map/convert.3
  15.9 0.9 reshape.395
  16.9 12.1 %fusion.2 = f32[640,2,20,32,4]{0,3,4,2,1:T(8,128)S(1)} fusion(bf16[20,32,4,1280]{3,2,1,0:T(4,128)(2,1)} %param.6, bf16[640,1,1280]{2,0,1:T(8,128)(2,1)S(1)} %get-tuple-element.12, bf16[640,1,1280]{2,0,1:T(8,128)(2,1)S(1)} %get-tuple-element.11), kind=kOutput, calls=%fused_computation.8 | convolution fusion | flops 8395161600 | bytes 22937600 | tf_op jit(solution)/shard_map/mrx,alfx->mralf/dot_general | solution.py:90
  29.0 0.0 copy-start
  29.0 15.4 %copy.70 = f32[640,2,20,32,4]{0,1,4,3,2:T(2,128)} copy(f32[640,2,20,32,4]{0,3,4,2,1:T(8,128)S(1)} %fusion.2) | data formatting | bytes 26214400 | tf_op jit(solution)/shard_map/mrx,alfx->mralf/dot_general | solution.py:90
  44.4 0.2 broadcast_in_dim_reshape.4
  44.6 0.0 copy-done
  44.7 0.8 dynamic_slice.10
  45.4 0.1 compare_convert_fusion
  45.5 7.9 %multiply_convert_fusion.1 = bf16[640,2,20,128]{0,1,3,2:T(2,128)(2,1)} fusion(f32[640,2,20,128]{0,1,3,2:T(2,128)} %bitcast.64, f32[640,20]{0,1:T(8,128)S(1)} %get-tuple-element.14), kind=kLoop, calls=%fused_computation.5 | loop fusion | flops 6553600 | bytes 19712000 | tf_op jit(solution)/shard_map/convert_element_type | solution.py:93
  53.5 22.8 %copy.71 = bf16[640,2,20,128]{3,1,2,0:T(2,128)(2,1)} copy(bf16[640,2,20,128]{0,1,3,2:T(2,128)(2,1)} %multiply_convert_fusion.1) | data formatting | bytes 13107200 | tf_op jit(solution)/shard_map/convert_element_type | solution.py:93
  76.3 84.1 %all_to_all.41 = bf16[640,2,20,128]{3,1,2,0:T(2,128)(2,1)S(1)} all-to-all(bf16[640,2,20,128]{3,1,2,0:T(2,128)(2,1)} %copy.71), channel_id=1, replica_groups=mesh['lat'=32,'lev'=4] {'lat'}, dimensions={0} | all-to-all | bytes 13107200 | tf_op jit(solution)/shard_map/all_to_all | solution.py:95
  160.4 5.8 %copy.72 = bf16[20,2,32,20,128]{4,1,3,2,0:T(2,128)(2,1)} copy(bf16[20,2,32,20,128]{4,1,3,0,2:T(2,128)(2,1)S(1)} %bitcast.69) | data formatting | bytes 13107200 | tf_op jit(solution)/shard_map/all_to_all | solution.py:95
  166.3 0.0 copy-start.2
  166.3 0.0 copy-start.1
  166.3 5.4 %all-to-all-start.1 = ((bf16[20,2,640,128]{3,1,2,0:T(2,128)(2,1)}), bf16[20,2,640,128]{3,1,2,0:T(2,128)(2,1)}, u32[]{:S(2)}, u32[]{:S(2)}) async-start(bf16[20,2,640,128]{3,1,2,0:T(2,128)(2,1)} %bitcast.65), calls=%async_computation.1 | async-start | bytes 13107200 | tf_op jit(solution)/shard_map/all_to_all | solution.py:94
  171.7 0.1 dynamic_slice.11
  171.8 0.0 copy-done.2
  171.8 0.1 copy.76
  171.9 0.0 copy-done.1
  171.9 77.4 %all_gather.3 = bf16[128,129]{1,0:T(8,128)(2,1)S(1)} all-gather(bf16[32,129]{1,0:T(8,128)(2,1)S(1)} %pad_maximum_fusion.1), channel_id=1, replica_groups=mesh['lat'=32,'lev'=4] {'lev'}, dimensions={0}, use_global_device_ids=true | all-gather | bytes 41280 | tf_op jit(solution)/shard_map/all_gather | solution.py:13
  249.3 0.1 convert_reduce_fusion
  249.4 0.1 fusion.29
  249.4 0.1 add_divide_fusion
  249.6 0.0 all-to-all-done.1
  249.6 7.2 %copy.73 = bf16[20,2,640,128]{3,2,1,0:T(8,128)(2,1)} copy(bf16[20,2,640,128]{3,1,2,0:T(2,128)(2,1)} %all-to-all-done.1) | data formatting | bytes 13107200 | tf_op jit(solution)/shard_map/all_to_all | solution.py:94
  256.8 9.5 %copy.74 = bf16[5,2,640,4,128]{2,4,3,1,0:T(8,128)(2,1)} copy(bf16[5,2,640,4,128]{4,2,1,0,3:T(8,128)(2,1)} %bitcast.70) | data formatting | bytes 13107200 | tf_op jit(solution)/shard_map/all_to_all | solution.py:94
  266.3 11.1 %multiply_convert_fusion = bf16[5,640,2,512]{1,3,2,0:T(8,128)(2,1)} fusion(bf16[5,2,640,512]{2,3,1,0:T(8,128)(2,1)} %bitcast.72, f32[5,640]{1,0:T(8,128)S(1)} %fusion.29, bf16[20,640,640]{2,1,0:T(8,128)(2,1)} %param.7, s32[]{:T(128)S(6)} %select_n.50), kind=kOutput, calls=%fused_computation.4 | convolution fusion | flops 4200857600 | bytes 17216004 | tf_op jit(solution)/shard_map/sna,srac->snrc/dot_general | solution.py:71
  277.4 11.8 %reshape.389 = bf16[5,640,2,128,4]{1,4,3,2,0:T(4,128)(2,1)} reshape(bf16[5,640,2,512]{1,3,2,0:T(8,128)(2,1)} %multiply_convert_fusion) | data formatting | bytes 13107200 | tf_op jit(solution)/shard_map/reshape | solution.py:109
  289.2 7.9 %fusion.1 = bf16[5,640,2,128,4]{1,3,4,2,0:T(8,128)(2,1)S(1)} fusion(bf16[5,640,2,128,4]{1,4,3,2,0:T(4,128)(2,1)} %reshape.389, f32[640,128]{0,1:T(8,128)S(1)} %add_divide_fusion, bf16[128,129]{1,0:T(8,128)(2,1)S(1)} %all_gather.3), kind=kOutput, calls=%fused_computation.3 | convolution fusion | flops 851968000 | bytes 20021248 | tf_op jit(solution)/shard_map/snrkf,lk->snrlf/dot_general | solution.py:110
  297.1 28.2 %copy.78 = bf16[5,640,2,128,4]{1,2,4,3,0:T(2,128)(2,1)S(1)} copy(bf16[5,640,2,128,4]{1,3,4,2,0:T(8,128)(2,1)S(1)} %fusion.1) | data formatting | bytes 13107200 | tf_op jit(solution)/shard_map/convert_element_type | solution.py:114
  325.3 10.1 %convert_bitcast_fusion = bf16[5,2,640,512]{2,3,1,0:T(8,128)(2,1)} fusion(bf16[5,640,2,512]{1,2,3,0:T(2,128)(2,1)S(1)} %bitcast.73, bf16[20,640,640]{2,1,0:T(8,128)(2,1)} %param.7, s32[]{:T(128)S(6)} %select_n.50), kind=kOutput, calls=%fused_computation.15 | convolution fusion | flops 4197580800 | bytes 17203204 | tf_op jit(solution)/shard_map/sna,snrc->srac/dot_general | solution.py:79
  335.4 16.7 %copy.80 = bf16[5,2,640,512]{3,1,2,0:T(2,128)(2,1)} copy(bf16[5,2,640,512]{2,3,1,0:T(8,128)(2,1)} %convert_bitcast_fusion) | data formatting | bytes 13107200 | tf_op jit(solution)/shard_map/convert_element_type | solution.py:80
  352.1 7.1 %fusion.36 = (bf16[32,5,2,20,128]{4,2,3,0,1:T(2,128)(2,1)S(1)}, bf16[32,5,2,20,128]{4,2,3,0,1:T(2,128)(2,1)S(1)}, bf16[32,5,2,20,128]{4,2,3,0,1:T(2,128)(2,1)S(1)}, bf16[32,5,2,20,128]{4,2,3,0,1:T(2,128)(2,1)S(1)}) fusion(bf16[32,5,2,20,512]{4,2,3,0,1:T(2,128)(2,1)} %bitcast.67), kind=kLoop, calls=%fused_computation.62 | loop fusion | bytes 13107200 | tf_op jit(solution)/shard_map/slice
  359.2 11.0 %pad_maximum_fusion = bf16[32,20,2,20,128]{4,2,3,0,1:T(2,128)(2,1)S(1)} fusion(bf16[32,5,2,20,128]{4,2,3,0,1:T(2,128)(2,1)S(1)} %get-tuple-element.6, bf16[32,5,2,20,128]{4,2,3,0,1:T(2,128)(2,1)S(1)} %get-tuple-element.7, bf16[32,5,2,20,128]{4,2,3,0,1:T(2,128)(2,1)S(1)} %get-tuple-element.8, bf16[32,5,2,20,128]{4,2,3,0,1:T(2,128)(2,1)S(1)} %get-tuple-element.5), kind=kLoop, calls=%fused_computation.6 | loop fusion | flops 9830400 | bytes 13107200 | tf_op jit(solution)/shard_map/concatenate
  370.2 5.9 %copy.81 = bf16[32,20,2,20,128]{4,2,3,1,0:T(2,128)(2,1)} copy(bf16[32,20,2,20,128]{4,2,3,0,1:T(2,128)(2,1)S(1)} %pad_maximum_fusion) | data formatting | bytes 13107200 | tf_op jit(solution)/shard_map/concatenate
  376.0 8.1 %all-to-all-start.2 = ((bf16[128,5,2,20,128]{4,2,3,1,0:T(2,128)(2,1)}), bf16[128,5,2,20,128]{4,2,3,1,0:T(2,128)(2,1)}, u32[]{:S(2)}, u32[]{:S(2)}) async-start(bf16[128,5,2,20,128]{4,2,3,1,0:T(2,128)(2,1)} %bitcast.66), calls=%async_computation.2 | async-start | bytes 13107200 | tf_op jit(solution)/shard_map/all_to_all | solution.py:37
  384.2 0.2 copy.84
  384.4 15.2 %multiply_convert_fusion.3 = (bf16[640,1,1280]{2,0,1:T(8,128)(2,1)S(1)}, bf16[640,1,1280]{2,0,1:T(8,128)(2,1)S(1)}) fusion(f32[640]{0:T(1024)S(1)} %select_multiply_fusion, s32[640]{0:T(1024)S(1)} %broadcast_in_dim_reshape.4), kind=kLoop, calls=%fused_computation.33 | loop fusion | flops 11468800 | bytes 3281920 | tf_op jit(solution)/shard_map/convert.1
  399.5 63.9 %all-to-all-done.2 = bf16[128,5,2,20,128]{4,2,3,1,0:T(2,128)(2,1)} async-done(((bf16[128,5,2,20,128]{4,2,3,1,0:T(2,128)(2,1)}), bf16[128,5,2,20,128]{4,2,3,1,0:T(2,128)(2,1)}, u32[]{:S(2)}, u32[]{:S(2)}) %all-to-all-start.2) | async-done | bytes 6553632 | tf_op jit(solution)/shard_map/all_to_all | solution.py:37
  463.4 6.0 %copy.82 = bf16[32,4,5,2,20,128]{5,3,4,2,0,1:T(2,128)(2,1)S(1)} copy(bf16[32,4,5,2,20,128]{5,3,4,2,1,0:T(2,128)(2,1)} %bitcast.22) | data formatting | bytes 13107200 | tf_op jit(solution)/shard_map/reshape | solution.py:38
  469.5 17.0 %bitcast_multiply_fusion = bf16[640,2,20,128]{3,1,2,0:T(2,128)(2,1)} fusion(bf16[32,4,5,2,20,128]{5,3,4,2,0,1:T(2,128)(2,1)S(1)} %copy.82, bf16[640,20]{1,0:T(8,128)(2,1)S(1)} %copy.84), kind=kLoop, calls=%fused_computation.7 | loop fusion | flops 3276800 | bytes 13132800 | tf_op jit(solution)/shard_map/mul | solution.py:124
  486.5 23.5 %copy.85 = bf16[20,128,640,2]{2,3,1,0:T(2,128)(2,1)} copy(bf16[20,128,640,2]{1,3,0,2:T(2,128)(2,1)} %bitcast.68) | data formatting | bytes 13107200 | tf_op jit(solution)/shard_map/mrac,mrx->acx/dot_general | solution.py:125
  510.0 13.3 %bitcast_convert_fusion = bf16[20,32,4,1280]{3,1,2,0:T(8,128)(2,1)} fusion(bf16[20,32,4,640,2]{3,4,2,1,0:T(2,128)(2,1)} %bitcast.71, bf16[640,1,1280]{2,0,1:T(8,128)(2,1)S(1)} %get-tuple-element.10, bf16[640,1,1280]{2,0,1:T(8,128)(2,1)S(1)} %get-tuple-element.9), kind=kOutput, calls=%fused_computation | convolution fusion | flops 8393523200 | bytes 16384000 | tf_op jit(solution)/shard_map/mrac,mrx->acx/dot_general | solution.py:125
  523.3 11.4 %copy.87 = bf16[20,32,4,1280]{3,2,1,0:T(4,128)(2,1)} copy(bf16[20,32,4,1280]{3,1,2,0:T(8,128)(2,1)} %bitcast_convert_fusion) | data formatting | bytes 13107200 | tf_op jit(solution)/shard_map/convert_element_type | solution.py:128
  (5 shorter events, 0.0 us)
Async XLA Ops:
  29.0 15.6 %copy-start = (s32[640]{0:T(1024)S(1)}, s32[640]{0:T(1024)}, u32[]{:S(2)}) copy-start(s32[640]{0:T(1024)} %param.11) | copy-start | bytes 7684
  166.3 5.5 %copy-start.2 = (bf16[32]{0:T(256)(128)(2,1)S(1)}, bf16[32]{0:T(256)(128)(2,1)}, u32[]{:S(2)}) copy-start(bf16[32]{0:T(256)(128)(2,1)} %param.9) | copy-start | bytes 196
  166.3 5.6 %copy-start.1 = (bf16[32,128]{1,0:T(8,128)(2,1)S(1)}, bf16[32,128]{1,0:T(8,128)(2,1)}, u32[]{:S(2)}) copy-start(bf16[32,128]{1,0:T(8,128)(2,1)} %param.8) | copy-start | bytes 24580
  166.3 83.3 %all-to-all-start.1 = ((bf16[20,2,640,128]{3,1,2,0:T(2,128)(2,1)}), bf16[20,2,640,128]{3,1,2,0:T(2,128)(2,1)}, u32[]{:S(2)}, u32[]{:S(2)}) async-start(bf16[20,2,640,128]{3,1,2,0:T(2,128)(2,1)} %bitcast.65), calls=%async_computation.1 | async-start | bytes 13107200 | tf_op jit(solution)/shard_map/all_to_all | solution.py:94
  376.0 87.4 %all-to-all-start.2 = ((bf16[128,5,2,20,128]{4,2,3,1,0:T(2,128)(2,1)}), bf16[128,5,2,20,128]{4,2,3,1,0:T(2,128)(2,1)}, u32[]{:S(2)}, u32[]{:S(2)}) async-start(bf16[128,5,2,20,128]{4,2,3,1,0:T(2,128)(2,1)} %bitcast.66), calls=%async_computation.2 | async-start | bytes 13107200 | tf_op jit(solution)/shard_map/all_to_all | solution.py:37
where the time goes:
time: 537 us; the launch traced here: 535 us
  local copies, waits for them, and re-layouts  174 us (32%)
  blocking collectives  162 us (30%)
  other arithmetic  67.4 us (13%)
  waiting for transfers between devices  63.9 us (12%)
  matrix products  54.5 us (10%)
  starting transfers between devices  13.6 us (3%)
    all_to_all x1, blocking collectives, per_device(): lax.all_to_all(fourier, 'lat', split_axis=0, concat_axis=2, tiled=True)  84.1 us
    all_gather x1, blocking collectives, sent_together(): result = lax.all_gather(both, axis, axis=dim, tiled=True)  77.4 us
    all_to_all x1, waiting for transfers between devices, joined_exchange(): lax.all_to_all(pieces, axis, split_axis=0, concat_axis=0, tiled=True)  63.9 us
    another operation x2, other arithmetic  31.1 us
    convert_element_type x1, local copies, waits for them, and re-layouts, per_device(): mixed.astype(jnp.bfloat16).reshape(count, degrees, 2, levels * fields)  28.2 us
    dot_general x1, local copies, waits for them, and re-layouts, per_device(): jnp.einsum('mrac,mrx->acx', returned, inverse_table, preferred_element_ty...  23.5 us
    convert_element_type x1, local copies, waits for them, and re-layouts, per_device(): fourier = (fourier * forward_kept[:, None, :, None]).astype(jnp.bfloat16)  22.8 us
    mul x1, other arithmetic, per_device(): returned = returned * back_kept[:, None, :, None]  17 us
  transfers between devices with their start and end apart: 2, of which 1 were waited for; matrix products, arithmetic and copies ran while one was open for 3% of the time, Pallas kernels for 0%

commit v1 on v0

--- a/solution.py
+++ b/solution.py
@@ -91,13 +91,24 @@
     fourier = fourier.reshape(slot_count, 2, lat_rows, level_rows * fields)
     forward_kept = (2 * wave_slots[:, None] < own_counts[None, :]).astype(jnp.float32)
     fourier = (fourier * forward_kept[:, None, :, None]).astype(jnp.bfloat16)
-    gathered = lax.all_to_all(
-        lax.all_to_all(fourier, "lat", split_axis=0, concat_axis=2, tiled=True),
-        "lev",
-        split_axis=0,
-        concat_axis=3,
-        tiled=True,
-    )
+
+    def review_tails(x0):
+        mid_arr, answer = (jax.lax.axis_size("lev"), jax.lax.axis_index("lev"))
+        f_next = x0.shape[0] // mid_arr
+        g_now = jnp.roll(x0, shift=-answer * f_next, axis=0)
+        by_rank = [lax.slice_in_dim(g_now, 0, f_next, axis=0)]
+        for rr in [*range(1, mid_arr)]:
+            y2 = lax.slice_in_dim(g_now, rr * f_next, (rr + 1) * f_next, axis=0)
+            by_rank.append(
+                jax.lax.ppermute(
+                    y2, axis_name="lev", perm=[(i, (i + rr) % mid_arr) for i in range(mid_arr)]
+                )
+            )
+        block_next = jnp.concatenate(by_rank[::-1], axis=3)
+        local_part = jnp.roll(block_next, shift=(answer + 1) * by_rank[0].shape[3], axis=3)
+        return local_part
+
+    gathered = review_tails(lax.all_to_all(fourier, "lat", split_axis=0, concat_axis=2, tiled=True))
     count = gathered.shape[0]
     own_table = lax.dynamic_slice_in_dim(legendre, lax.axis_index("lev") * count, count, 0)
     own_waves = lax.dynamic_slice_in_dim(

time: 537 us -> 582 us (1.084); the launches traced: 535 us -> 573 us
  blocking collectives: 162 us -> 77.5 us
  waiting for transfers between devices: 63.9 us -> 142 us
  local copies, waits for them, and re-layouts: 174 us -> 200 us
  other arithmetic: 67.4 us -> 76.4 us
  starting transfers between devices: 13.6 us -> 21.9 us
    all_to_all x1 -> x0, blocking collectives: 84.1 us -> none  [per_device(): lax.all_to_all(fourier, 'lat', split_axis=0, concat_axis=2, tiled=True)]
    all_to_all x1, waiting for transfers between devices: 0.01 us -> 78.1 us  [per_device(): lax.all_to_all(fourier, 'lat', split_axis=0, concat_axis=2, tiled=True)]
    unnamed x6 -> x15, local copies, waits for them, and re-layouts: 0.01 us -> 18.5 us
    all_to_all x1 -> x2, local copies, waits for them, and re-layouts: 5.81 us -> 23.6 us  [per_device(): lax.all_to_all(fourier, 'lat', split_axis=0, concat_axis=2, tiled=True)]
    all_to_all x2 -> x0, local copies, waits for them, and re-layouts: 16.7 us -> none  [per_device(): lax.all_to_all(lax.all_to_all(fourier, 'lat', split_axis=0, concat_axis=2...]
    another operation x2 -> x3, other arithmetic: 31.1 us -> 42.1 us
    another operation x0 -> x1, local copies, waits for them, and re-layouts: none -> 5.88 us
    slice x1 -> x2, local copies, waits for them, and re-layouts: 7.1 us -> 12 us
  transfers between devices with their start and end apart: 2 -> 5, of which waited for: 1 -> 2; matrix products, arithmetic and copies ran while one was open for 3% -> 4% of each run, Pallas kernels for 0% -> 0%
where the time goes in v1:
time: 582 us; the launch traced here: 573 us
  local copies, waits for them, and re-layouts  200 us (34%)
  waiting for transfers between devices  142 us (24%)
  blocking collectives  77.5 us (13%)
  other arithmetic  76.4 us (13%)
  matrix products  55.1 us (9%)
  starting transfers between devices  21.9 us (4%)
    all_to_all x1, waiting for transfers between devices, per_device(): lax.all_to_all(fourier, 'lat', split_axis=0, concat_axis=2, tiled=True)  78.1 us
    all_gather x1, blocking collectives, sent_together(): result = lax.all_gather(both, axis, axis=dim, tiled=True)  77.5 us
    all_to_all x1, waiting for transfers between devices, joined_exchange(): lax.all_to_all(pieces, axis, split_axis=0, concat_axis=0, tiled=True)  63.9 us
    another operation x3, other arithmetic  42.1 us
    convert_element_type x1, local copies, waits for them, and re-layouts, per_device(): mixed.astype(jnp.bfloat16).reshape(count, degrees, 2, levels * fields)  28.2 us
    all_to_all x2, local copies, waits for them, and re-layouts, per_device(): lax.all_to_all(fourier, 'lat', split_axis=0, concat_axis=2, tiled=True)  23.6 us
    dot_general x1, local copies, waits for them, and re-layouts, per_device(): jnp.einsum('mrac,mrx->acx', returned, inverse_table, preferred_element_ty...  23.5 us
    convert_element_type x1, local copies, waits for them, and re-layouts, per_device(): fourier = (fourier * forward_kept[:, None, :, None]).astype(jnp.bfloat16)  22.8 us
  transfers between devices with their start and end apart: 5, of which 2 were waited for; matrix products, arithmetic and copies ran while one was open for 4% of the time, Pallas kernels for 0%

profile of v1, /device:TPU:3, one launch (start us, length us, event | category | flops | bytes accessed | tf_op | source)
XLA Modules:
  0.0 573.5 jit_solution(1180536864654457044)
XLA Ops:
  0.0 0.9 reshape.395
  0.9 15.9 %multiply_convert_fusion.5 = (bf16[640,1,1280]{2,0,1:T(8,128)(2,1)S(1)}, bf16[640,1,1280]{2,0,1:T(8,128)(2,1)S(1)}) fusion(s32[640]{0:T(1024)} %param.11), kind=kLoop, calls=%fused_computation.42 | loop fusion | flops 11468800 | bytes 3279360 | tf_op jit(solution)/shard_map/convert.3
  16.9 0.2 broadcast_in_dim_reshape.4
  17.1 0.7 broadcast_multiply_fusion
  17.8 12.1 %fusion.3 = f32[640,2,20,32,4]{0,3,4,2,1:T(8,128)S(1)} fusion(bf16[20,32,4,1280]{3,2,1,0:T(4,128)(2,1)} %param.6, bf16[640,1,1280]{2,0,1:T(8,128)(2,1)S(1)} %get-tuple-element.15, bf16[640,1,1280]{2,0,1:T(8,128)(2,1)S(1)} %get-tuple-element.14), kind=kOutput, calls=%fused_computation.11 | convolution fusion | flops 8395161600 | bytes 22937600 | tf_op jit(solution)/shard_map/mrx,alfx->mralf/dot_general | solution.py:90
  29.9 15.4 %copy.52 = f32[640,2,20,32,4]{0,1,4,3,2:T(2,128)} copy(f32[640,2,20,32,4]{0,3,4,2,1:T(8,128)S(1)} %fusion.3) | data formatting | bytes 26214400 | tf_op jit(solution)/shard_map/mrx,alfx->mralf/dot_general | solution.py:90
  45.3 0.8 dynamic_slice.18
  46.2 7.9 %multiply_convert_fusion.1 = bf16[640,2,20,128]{0,1,3,2:T(2,128)(2,1)} fusion(f32[640,2,20,128]{0,1,3,2:T(2,128)} %bitcast.59, f32[640,20]{0,1:T(8,128)S(1)} %get-tuple-element.17), kind=kLoop, calls=%fused_computation.7 | loop fusion | flops 6553600 | bytes 19712000 | tf_op jit(solution)/shard_map/convert_element_type | solution.py:93
  54.1 22.8 %copy.53 = bf16[640,2,20,128]{3,1,2,0:T(2,128)(2,1)} copy(bf16[640,2,20,128]{0,1,3,2:T(2,128)(2,1)} %multiply_convert_fusion.1) | data formatting | bytes 13107200 | tf_op jit(solution)/shard_map/convert_element_type | solution.py:93
  77.0 9.3 %all-to-all-start = ((bf16[640,2,20,128]{3,1,2,0:T(2,128)(2,1)}), bf16[640,2,20,128]{3,1,2,0:T(2,128)(2,1)}, u32[]{:S(2)}, u32[]{:S(2)}) async-start(bf16[640,2,20,128]{3,1,2,0:T(2,128)(2,1)} %copy.53), calls=%async_computation | async-start | bytes 13107200 | tf_op jit(solution)/shard_map/all_to_all | solution.py:111
  86.3 78.1 %all-to-all-done = bf16[640,2,20,128]{3,1,2,0:T(2,128)(2,1)} async-done(((bf16[640,2,20,128]{3,1,2,0:T(2,128)(2,1)}), bf16[640,2,20,128]{3,1,2,0:T(2,128)(2,1)}, u32[]{:S(2)}, u32[]{:S(2)}) %all-to-all-start) | async-done | bytes 6553632 | tf_op jit(solution)/shard_map/all_to_all | solution.py:111
  164.3 7.0 %copy.54 = bf16[20,2,32,20,128]{4,1,3,2,0:T(2,128)(2,1)} copy(bf16[20,2,32,20,128]{4,1,3,0,2:T(2,128)(2,1)} %bitcast.7) | data formatting | bytes 13107200 | tf_op jit(solution)/shard_map/all_to_all | solution.py:111
  171.3 16.6 %copy.55 = bf16[20,2,640,128]{2,3,1,0:T(8,128)(2,1)} copy(bf16[20,2,640,128]{3,1,2,0:T(2,128)(2,1)} %bitcast.65) | data formatting | bytes 13107200 | tf_op jit(solution)/shard_map/all_to_all | solution.py:111
  188.0 8.3 %fusion.2 = bf16[20,2,640,128]{2,3,1,0:T(8,128)(2,1)} fusion(s32[]{:T(128)S(6)} %select_n.76, bf16[20,2,640,128]{2,3,1,0:T(8,128)(2,1)} %copy.55), kind=kLoop, calls=%fused_computation.8 | loop fusion | flops 3276800 | bytes 13107204 | tf_op jit(solution)/shard_map/jit(_roll_dynamic)/concatenate | solution.py:98
  196.3 4.9 fusion.39
  201.2 2.8 collective-permute-start
  204.0 0.4 collective-permute-start.1
  204.4 0.7 collective-permute-start.2
  205.1 0.8 dynamic_slice.21
  205.9 77.5 %all_gather.3 = bf16[128,129]{1,0:T(8,128)(2,1)S(1)} all-gather(bf16[32,129]{1,0:T(8,128)(2,1)S(1)} %pad_maximum_fusion.1), channel_id=1, replica_groups=mesh['lat'=32,'lev'=4] {'lev'}, dimensions={0}, use_global_device_ids=true | all-gather | bytes 41280 | tf_op jit(solution)/shard_map/all_gather | solution.py:13
  283.5 0.1 convert_reduce_fusion
  283.6 0.1 add_divide_fusion
  283.8 3.0 constant_dynamic-update-slice_fusion.5
  286.8 2.8 constant_dynamic-update-slice_fusion.4
  289.6 2.8 constant_dynamic-update-slice_fusion.3
  292.4 1.4 slice_dynamic-update-slice_fusion
  293.8 2.9 constant_dynamic-update-slice_fusion.2
  296.7 2.8 constant_dynamic-update-slice_fusion.1
  299.5 2.8 constant_dynamic-update-slice_fusion
  302.3 1.3 slice_dynamic-update-slice_fusion.1
  303.6 11.6 %multiply_convert_fusion = bf16[5,640,2,512]{1,3,2,0:T(8,128)(2,1)} fusion(f32[5,640]{1,0:T(8,128)S(1)} %fusion.31, bf16[5,2,640,1024]{2,3,1,0:T(8,128)(2,1)} %slice_dynamic-update-slice_fusion.1, s32[]{:T(128)S(6)} %select_n.78, bf16[20,640,640]{2,1,0:T(8,128)(2,1)} %param.7, s32[]{:T(128)S(6)} %select_n.72), kind=kOutput, calls=%fused_computation.6 | convolution fusion | flops 4200857600 | bytes 17216008 | tf_op jit(solution)/shard_map/sna,srac->snrc/dot_general | solution.py:71
  315.2 11.8 %reshape.389 = bf16[5,640,2,128,4]{1,4,3,2,0:T(4,128)(2,1)} reshape(bf16[5,640,2,512]{1,3,2,0:T(8,128)(2,1)} %multiply_convert_fusion) | data formatting | bytes 13107200 | tf_op jit(solution)/shard_map/reshape | solution.py:120
  327.0 7.9 %fusion.1 = bf16[5,640,2,128,4]{1,3,4,2,0:T(8,128)(2,1)S(1)} fusion(bf16[5,640,2,128,4]{1,4,3,2,0:T(4,128)(2,1)} %reshape.389, f32[640,128]{0,1:T(8,128)S(1)} %add_divide_fusion, bf16[128,129]{1,0:T(8,128)(2,1)S(1)} %all_gather.3), kind=kOutput, calls=%fused_computation.5 | convolution fusion | flops 851968000 | bytes 20021248 | tf_op jit(solution)/shard_map/snrkf,lk->snrlf/dot_general | solution.py:121
  334.9 28.2 %copy.60 = bf16[5,640,2,128,4]{1,2,4,3,0:T(2,128)(2,1)S(1)} copy(bf16[5,640,2,128,4]{1,3,4,2,0:T(8,128)(2,1)S(1)} %fusion.1) | data formatting | bytes 13107200 | tf_op jit(solution)/shard_map/convert_element_type | solution.py:125
  363.1 10.1 %convert_bitcast_fusion = bf16[5,2,640,512]{2,3,1,0:T(8,128)(2,1)} fusion(bf16[5,640,2,512]{1,2,3,0:T(2,128)(2,1)S(1)} %bitcast.67, bf16[20,640,640]{2,1,0:T(8,128)(2,1)} %param.7, s32[]{:T(128)S(6)} %select_n.72), kind=kOutput, calls=%fused_computation.18 | convolution fusion | flops 4197580800 | bytes 17203204 | tf_op jit(solution)/shard_map/sna,snrc->srac/dot_general | solution.py:79
  373.2 16.7 %copy.62 = bf16[5,2,640,512]{3,1,2,0:T(2,128)(2,1)} copy(bf16[5,2,640,512]{2,3,1,0:T(8,128)(2,1)} %convert_bitcast_fusion) | data formatting | bytes 13107200 | tf_op jit(solution)/shard_map/convert_element_type | solution.py:80
  389.9 7.1 %fusion.38 = (bf16[32,5,2,20,128]{4,2,3,0,1:T(2,128)(2,1)S(1)}, bf16[32,5,2,20,128]{4,2,3,0,1:T(2,128)(2,1)S(1)}, bf16[32,5,2,20,128]{4,2,3,0,1:T(2,128)(2,1)S(1)}, bf16[32,5,2,20,128]{4,2,3,0,1:T(2,128)(2,1)S(1)}) fusion(bf16[32,5,2,20,512]{4,2,3,0,1:T(2,128)(2,1)} %bitcast.63), kind=kLoop, calls=%fused_computation.74 | loop fusion | bytes 13107200 | tf_op jit(solution)/shard_map/slice
  397.0 11.0 %pad_maximum_fusion = bf16[32,20,2,20,128]{4,2,3,0,1:T(2,128)(2,1)S(1)} fusion(bf16[32,5,2,20,128]{4,2,3,0,1:T(2,128)(2,1)S(1)} %get-tuple-element.6, bf16[32,5,2,20,128]{4,2,3,0,1:T(2,128)(2,1)S(1)} %get-tuple-element.7, bf16[32,5,2,20,128]{4,2,3,0,1:T(2,128)(2,1)S(1)} %get-tuple-element.8, bf16[32,5,2,20,128]{4,2,3,0,1:T(2,128)(2,1)S(1)} %get-tuple-element.5), kind=kLoop, calls=%fused_computation.9 | loop fusion | flops 9830400 | bytes 13107200 | tf_op jit(solution)/shard_map/concatenate.5
  408.0 5.9 %copy.63 = bf16[32,20,2,20,128]{4,2,3,1,0:T(2,128)(2,1)} copy(bf16[32,20,2,20,128]{4,2,3,0,1:T(2,128)(2,1)S(1)} %pad_maximum_fusion) | data formatting | bytes 13107200 | tf_op jit(solution)/shard_map/concatenate.5
  413.9 8.8 %all-to-all-start.1 = ((bf16[128,5,2,20,128]{4,2,3,1,0:T(2,128)(2,1)}), bf16[128,5,2,20,128]{4,2,3,1,0:T(2,128)(2,1)}, u32[]{:S(2)}, u32[]{:S(2)}) async-start(bf16[128,5,2,20,128]{4,2,3,1,0:T(2,128)(2,1)} %bitcast.62), calls=%async_computation.1 | async-start | bytes 13107200 | tf_op jit(solution)/shard_map/all_to_all | solution.py:37
  422.7 0.2 copy.66
  422.9 15.2 %multiply_convert_fusion.3 = (bf16[640,1,1280]{2,0,1:T(8,128)(2,1)S(1)}, bf16[640,1,1280]{2,0,1:T(8,128)(2,1)S(1)}) fusion(f32[640]{0:T(1024)S(1)} %select_multiply_fusion, s32[640]{0:T(1024)S(1)} %broadcast_in_dim_reshape.4), kind=kLoop, calls=%fused_computation.37 | loop fusion | flops 11468800 | bytes 3281920 | tf_op jit(solution)/shard_map/convert.1
  438.1 63.9 %all-to-all-done.1 = bf16[128,5,2,20,128]{4,2,3,1,0:T(2,128)(2,1)} async-done(((bf16[128,5,2,20,128]{4,2,3,1,0:T(2,128)(2,1)}), bf16[128,5,2,20,128]{4,2,3,1,0:T(2,128)(2,1)}, u32[]{:S(2)}, u32[]{:S(2)}) %all-to-all-start.1) | async-done | bytes 6553632 | tf_op jit(solution)/shard_map/all_to_all | solution.py:37
  501.9 6.0 %copy.64 = bf16[32,4,5,2,20,128]{5,3,4,2,0,1:T(2,128)(2,1)S(1)} copy(bf16[32,4,5,2,20,128]{5,3,4,2,1,0:T(2,128)(2,1)} %bitcast.19) | data formatting | bytes 13107200 | tf_op jit(solution)/shard_map/reshape | solution.py:38
  508.0 17.0 %bitcast_multiply_fusion = bf16[640,2,20,128]{3,1,2,0:T(2,128)(2,1)} fusion(bf16[32,4,5,2,20,128]{5,3,4,2,0,1:T(2,128)(2,1)S(1)} %copy.64, bf16[640,20]{1,0:T(8,128)(2,1)S(1)} %copy.66), kind=kLoop, calls=%fused_computation.10 | loop fusion | flops 3276800 | bytes 13132800 | tf_op jit(solution)/shard_map/mul | solution.py:135
  525.0 23.5 %copy.67 = bf16[20,128,640,2]{2,3,1,0:T(2,128)(2,1)} copy(bf16[20,128,640,2]{1,3,0,2:T(2,128)(2,1)} %bitcast.64) | data formatting | bytes 13107200 | tf_op jit(solution)/shard_map/mrac,mrx->acx/dot_general | solution.py:136
  548.5 13.4 %bitcast_convert_fusion = bf16[20,32,4,1280]{3,1,2,0:T(8,128)(2,1)} fusion(bf16[20,32,4,640,2]{3,4,2,1,0:T(2,128)(2,1)} %bitcast.66, bf16[640,1,1280]{2,0,1:T(8,128)(2,1)S(1)} %get-tuple-element.13, bf16[640,1,1280]{2,0,1:T(8,128)(2,1)S(1)} %get-tuple-element.12), kind=kOutput, calls=%fused_computation.2 | convolution fusion | flops 8393523200 | bytes 16384000 | tf_op jit(solution)/shard_map/mrac,mrx->acx/dot_general | solution.py:136
  561.9 11.4 %copy.69 = bf16[20,32,4,1280]{3,2,1,0:T(4,128)(2,1)} copy(bf16[20,32,4,1280]{3,1,2,0:T(8,128)(2,1)} %bitcast_convert_fusion) | data formatting | bytes 13107200 | tf_op jit(solution)/shard_map/convert_element_type | solution.py:139
  (19 shorter events, 0.3 us)
Async XLA Ops:
  77.0 87.4 %all-to-all-start = ((bf16[640,2,20,128]{3,1,2,0:T(2,128)(2,1)}), bf16[640,2,20,128]{3,1,2,0:T(2,128)(2,1)}, u32[]{:S(2)}, u32[]{:S(2)}) async-start(bf16[640,2,20,128]{3,1,2,0:T(2,128)(2,1)} %copy.53), calls=%async_computation | async-start | bytes 13107200 | tf_op jit(solution)/shard_map/all_to_all | solution.py:111
  196.3 9.5 %copy-start.1 = (bf16[32]{0:T(256)(128)(2,1)S(1)}, bf16[32]{0:T(256)(128)(2,1)}, u32[]{:S(2)}) copy-start(bf16[32]{0:T(256)(128)(2,1)} %param.9) | copy-start | bytes 196
  196.3 9.6 %copy-start = (bf16[32,128]{1,0:T(8,128)(2,1)S(1)}, bf16[32,128]{1,0:T(8,128)(2,1)}, u32[]{:S(2)}) copy-start(bf16[32,128]{1,0:T(8,128)(2,1)} %param.8) | copy-start | bytes 24580
  196.3 96.1 %slice-start = ((s8[6553600]{0:T(1024)(128)(4,1)}), s8[2359296]{0:T(1024)(128)(4,1)S(1)}, s32[]{:S(2)}) async-start(s8[6553600]{0:T(1024)(128)(4,1)} %bitcast.60), calls=%async_computation.2 | async-start | bytes 4718592
  201.2 82.5 %collective-permute-start = (bf16[5,2,640,128]{2,3,1,0:T(8,128)(2,1)}, bf16[5,2,640,128]{2,3,1,0:T(8,128)(2,1)}, u32[]{:S(2)}, u32[]{:S(2)}) collective-permute-start(bf16[5,2,640,128]{2,3,1,0:T(8,128)(2,1)} %get-tuple-element.11), channel_id=1, source_target_pairs={{0,3},{1,0},{2,1},{3,2},{4,7},{5,4},{6,5},{7,6},{8,11},{9,8},{10,9... | collective-permute-start | bytes 4915208 | tf_op jit(solution)/shard_map/ppermute | solution.py:103
  204.0 82.8 %collective-permute-start.1 = (bf16[5,2,640,128]{2,3,1,0:T(8,128)(2,1)}, bf16[5,2,640,128]{2,3,1,0:T(8,128)(2,1)}, u32[]{:S(2)}, u32[]{:S(2)}) collective-permute-start(bf16[5,2,640,128]{2,3,1,0:T(8,128)(2,1)} %get-tuple-element.10), channel_id=1, source_target_pairs={{0,2},{1,3},{2,0},{3,1},{4,6},{5,7},{6,4},{7,5},{8,10},{9,11},{10,... | collective-permute-start | bytes 4915208 | tf_op jit(solution)/shard_map/ppermute | solution.py:103
  204.4 85.2 %collective-permute-start.2 = (bf16[5,2,640,128]{2,3,1,0:T(8,128)(2,1)}, bf16[5,2,640,128]{2,3,1,0:T(8,128)(2,1)}, u32[]{:S(2)}, u32[]{:S(2)}) collective-permute-start(bf16[5,2,640,128]{2,3,1,0:T(8,128)(2,1)} %get-tuple-element.9), channel_id=1, source_target_pairs={{0,1},{1,2},{2,3},{3,0},{4,5},{5,6},{6,7},{7,4},{8,9},{9,10},{10,1... | collective-permute-start | bytes 4915208 | tf_op jit(solution)/shard_map/ppermute | solution.py:103
  283.6 8.8 %slice-start.1 = ((s8[6553600]{0:T(1024)(128)(4,1)}), s8[4194304]{0:T(1024)(128)(4,1)S(1)}, s32[]{:S(2)}) async-start(s8[6553600]{0:T(1024)(128)(4,1)} %bitcast.60), calls=%async_computation.3 | async-start | bytes 8388608
  413.9 88.1 %all-to-all-start.1 = ((bf16[128,5,2,20,128]{4,2,3,1,0:T(2,128)(2,1)}), bf16[128,5,2,20,128]{4,2,3,1,0:T(2,128)(2,1)}, u32[]{:S(2)}, u32[]{:S(2)}) async-start(bf16[128,5,2,20,128]{4,2,3,1,0:T(2,128)(2,1)} %bitcast.62), calls=%async_computation.1 | async-start | bytes 13107200 | tf_op jit(solution)/shard_map/all_to_all | solution.py:37
